TPU v7x, 32 devices: a whole 2x2x4 slice. The times are simulated.
32 devices in a mesh: seq: 8 (over y, x, core), head: 4 (over z).
Axes of the slice: x: 2, y: 2, z: 4, core: 2. Of those that a mesh axis runs over, the one named last changes fastest.
Arguments:
- latent: bfloat16 [1024, 1024], P('seq'), may hold values from -15 to 15
- probe: bfloat16 [1024, 1024], P('seq'), may hold values from -6 to 6
- time_embed: float32 [1024], replicated, may hold values from -6 to 6
- gain_attn: float32 [1024], replicated, may hold values from 0.1 to 1.9
- w_query: bfloat16 [1024, 1024], P(None, 'head'), may hold values from -0.625 to 0.625
- w_key: bfloat16 [1024, 1024], P(None, 'head'), may hold values from -11 to 11
- w_value: bfloat16 [1024, 1024], P(None, 'head'), may hold values from -0.1875 to 0.1875
- w_out: bfloat16 [1024, 1024], P('head'), may hold values from -0.1875 to 0.1875
- gain_mlp: float32 [1024], replicated, may hold values from 0.1 to 1.9
- w_in: bfloat16 [1024, 4096], P(None, 'head'), may hold values from -0.1875 to 0.1875
- w_down: bfloat16 [4096, 1024], P('head'), may hold values from -0.09375 to 0.09375
Outputs:
- latent_end: float32 [1024, 1024], P('seq')
- frame_trace: float32 [1024], P('seq')
- frame_logp: float32 [1024], P('seq')
- mean_logp: float32 [], replicated
All inputs are finite; a program needn't handle non-finite values.
Results may differ from a plain program's by a relative error of at most 0.03.
The roundings to bfloat16 on the way count: a program that leaves them out, or rounds other values in their place, can miss the bound.
Values may be sent and summed in bfloat16 or wider, within the bound.
A program may use at most 64 MiB of HBM per device.

v0:
```python
import math
import jax
import jax.numpy as jnp
from jax import lax
from jax.sharding import PartitionSpec as P

HEAD_DIM = 64
STEPS = 2
EPSILON = 1e-05
GELU_COEF = 0.044715
ROOT_TWO_PI = math.sqrt(2.0 / math.pi)


def norm_pair(values, tangent, norm_gain):
    meansq = jnp.mean(values * values, axis=-1, keepdims=True) + EPSILON
    inverse = lax.rsqrt(meansq)
    inner_mean = jnp.mean(values * tangent, axis=-1, keepdims=True)
    primal = values * inverse * norm_gain
    derived = (tangent * inverse - values * inverse**3 * inner_mean) * norm_gain
    return (primal.astype(jnp.bfloat16), derived.astype(jnp.bfloat16))


def gelu_pair(pre_act, tangent):
    cubic_arg = pre_act + GELU_COEF * pre_act**3
    tanh_value = jnp.tanh(ROOT_TWO_PI * cubic_arg)
    output = 0.5 * pre_act * (1.0 + tanh_value)
    slope_value = 0.5 * (1.0 + tanh_value) + 0.5 * pre_act * (
        1.0 - tanh_value * tanh_value
    ) * ROOT_TWO_PI * (1.0 + 3.0 * GELU_COEF * pre_act * pre_act)
    return (output.astype(jnp.bfloat16), (slope_value * tangent).astype(jnp.bfloat16))


def split_heads(matrix):
    return matrix.reshape(matrix.shape[0], -1, HEAD_DIM)


def score_pair(queries, query_tang, keys, key_tang):
    scale = HEAD_DIM ** (-0.5)
    scores = jnp.einsum("rhd,shd->hrs", queries, keys, preferred_element_type=jnp.float32) * scale
    score_tang = (
        jnp.einsum("rhd,shd->hrs", query_tang, keys, preferred_element_type=jnp.float32)
        + jnp.einsum("rhd,shd->hrs", queries, key_tang, preferred_element_type=jnp.float32)
    ) * scale
    return (scores, score_tang)


def attention(queries, query_tang, keys, vals, key_tang, val_tang):
    rows = queries.shape[0]
    local_cols = queries.shape[1]
    head_count = local_cols // HEAD_DIM
    query_heads = split_heads(queries)
    query_tang_heads = split_heads(query_tang)
    top_start = jnp.full((head_count, rows), -1e30, jnp.float32)
    piece = (
        lax.all_gather(keys, "seq", axis=0, tiled=True),
        lax.all_gather(vals, "seq", axis=0, tiled=True),
    )
    keys_piece = split_heads(piece[0])
    vals_piece = split_heads(piece[1])
    scale = HEAD_DIM ** (-0.5)
    scores = (
        jnp.einsum("rhd,shd->hrs", query_heads, keys_piece, preferred_element_type=jnp.float32)
        * scale
    )
    new_top = jnp.maximum(top_start, jnp.max(scores, axis=-1))
    weights = jnp.exp(scores - new_top[:, :, None])
    total = jnp.sum(weights, axis=-1)
    add_primal = jnp.einsum(
        "hrs,shd->rhd", weights.astype(jnp.bfloat16), vals_piece, preferred_element_type=jnp.float32
    )
    row_top, total, acc_primal = (new_top, total, add_primal)
    piece = (
        lax.all_gather(keys, "seq", axis=0, tiled=True),
        lax.all_gather(vals, "seq", axis=0, tiled=True),
        lax.all_gather(key_tang, "seq", axis=0, tiled=True),
        lax.all_gather(val_tang, "seq", axis=0, tiled=True),
    )
    keys_piece = split_heads(piece[0])
    vals_piece = split_heads(piece[1])
    key_tang_piece = split_heads(piece[2])
    val_tang_piece = split_heads(piece[3])
    scores, score_tang = score_pair(query_heads, query_tang_heads, keys_piece, key_tang_piece)
    weights = jnp.exp(scores - row_top[:, :, None])
    weighted = weights * score_tang
    rounded = weights.astype(jnp.bfloat16)
    rounded_tang = weighted.astype(jnp.bfloat16)
    add_tang = jnp.einsum(
        "hrs,shd->rhd", rounded_tang, vals_piece, preferred_element_type=jnp.float32
    ) + jnp.einsum("hrs,shd->rhd", rounded, val_tang_piece, preferred_element_type=jnp.float32)
    carried = jnp.sum(weighted, axis=-1)
    total_t = jnp.transpose(total)[:, :, None]
    carried_t = jnp.transpose(carried)[:, :, None]
    primal = acc_primal / total_t
    tangent = add_tang / total_t - carried_t / total_t * primal
    return (
        primal.reshape(rows, local_cols).astype(jnp.bfloat16),
        tangent.reshape(rows, local_cols).astype(jnp.bfloat16),
    )


def attend_rows(normed, normed_tang, w_query, w_key, w_value):
    rows = normed.shape[0]
    stacked = jnp.concatenate([normed, normed_tang], axis=0)

    def project(weight):
        both = jnp.dot(stacked, weight, preferred_element_type=jnp.float32).astype(jnp.bfloat16)
        return (both[:rows], both[rows:])

    queries, query_tang = project(w_query)
    keys, key_tang = project(w_key)
    vals, val_tang = project(w_value)
    return attention(queries, query_tang, keys, vals, key_tang, val_tang)


def hidden_pair(normed_mlp, normed_mlp_tang, w_in):
    rows = normed_mlp.shape[0]
    pre_both = jnp.dot(
        jnp.concatenate([normed_mlp, normed_mlp_tang], axis=0),
        w_in,
        preferred_element_type=jnp.float32,
    )
    return gelu_pair(pre_both[:rows], pre_both[rows:])


def whole_field(
    inputs, direction, gain_attn, w_query, w_key, w_value, w_out, gain_mlp, w_in, w_down
):
    rows = inputs.shape[0]
    normed, normed_tang = norm_pair(inputs, direction, gain_attn)
    head_out, head_tang = attend_rows(normed, normed_tang, w_query, w_key, w_value)
    attn_terms = jnp.dot(
        jnp.concatenate([head_out, head_tang], axis=0), w_out, preferred_element_type=jnp.float32
    )
    attn_both = lax.psum(attn_terms, "head")
    attn = attn_both[:rows]
    attn_tang = attn_both[rows:]
    middle = inputs + attn
    middle_tang = direction + attn_tang
    normed_mlp, normed_mlp_tang = norm_pair(middle, middle_tang, gain_mlp)
    activ, activ_tang = hidden_pair(normed_mlp, normed_mlp_tang, w_in)
    mlp_terms = jnp.dot(
        jnp.concatenate([activ, activ_tang], axis=0), w_down, preferred_element_type=jnp.float32
    )
    mlp_both = lax.psum(mlp_terms, "head")
    return (attn + mlp_both[:rows], attn_tang + mlp_both[rows:])


def per_device(
    latent, probe, time_embed, gain_attn, w_query, w_key, w_value, w_out, gain_mlp, w_in, w_down
):
    rows = latent.shape[0]
    width = latent.shape[1]
    state = latent.astype(jnp.float32)
    direction = probe.astype(jnp.float32)
    trace = jnp.zeros((rows,), jnp.float32)
    for euler_step in range(STEPS):
        inputs = state + euler_step / STEPS * time_embed
        field, field_tang = whole_field(
            inputs, direction, gain_attn, w_query, w_key, w_value, w_out, gain_mlp, w_in, w_down
        )
        trace = trace + jnp.sum(direction * field_tang, axis=-1) / (STEPS * width)
        state = state + field / STEPS
    frame_logp = (
        trace - 0.5 * jnp.sum(state * state, axis=-1) / width - 0.5 * math.log(2.0 * math.pi)
    )
    grand_total = lax.psum(jnp.sum(frame_logp), "seq")
    mean_logp = grand_total / (rows * lax.axis_size("seq"))
    return (state, trace, frame_logp, mean_logp)


def solution(mesh):
    return jax.shard_map(
        per_device,
        mesh=mesh,
        in_specs=(
            P("seq", None),
            P("seq", None),
            P(),
            P(),
            P(None, "head"),
            P(None, "head"),
            P(None, "head"),
            P("head", None),
            P(),
            P(None, "head"),
            P("head", None),
        ),
        out_specs=(P("seq", None), P("seq"), P("seq"), P()),
        check_vma=False,
    )
```

profile of v0, /device:TPU:0, one launch (start us, length us, event | category | flops | bytes accessed | tf_op | source)
XLA Modules:
  0.0 390.4 jit_solution(14046082699471560486)
XLA Ops:
  12.2 11.3 %all_gather.29 = bf16[1024,256]{1,0:T(8,128)(2,1)S(1)} all-gather(bf16[128,256]{1,0:T(8,128)(2,1)S(1)} %get-tuple-element.42), channel_id=1, replica_groups=mesh['seq'=8,'head'=4] {'seq'}, dimensions={0}, use_global_device_ids=true | all-gather | bytes 589824 | tf_op jit(solution)/shard_map/all_gather | solution.py:55
  28.9 9.8 %all_gather.30 = bf16[1024,256]{1,0:T(8,128)(2,1)S(1)} all-gather(bf16[128,256]{1,0:T(8,128)(2,1)S(1)} %get-tuple-element.41), channel_id=1, replica_groups=mesh['seq'=8,'head'=4] {'seq'}, dimensions={0}, use_global_device_ids=true | all-gather | bytes 589824 | tf_op jit(solution)/shard_map/all_gather | solution.py:75
  40.4 9.9 %all_gather.28 = bf16[1024,256]{1,0:T(8,128)(2,1)} all-gather(bf16[128,256]{1,0:T(8,128)(2,1)S(1)} %get-tuple-element.40), channel_id=1, replica_groups=mesh['seq'=8,'head'=4] {'seq'}, dimensions={0}, use_global_device_ids=true | all-gather | bytes 589824 | tf_op jit(solution)/shard_map/all_gather | solution.py:56
  51.6 2.2 fusion
  53.9 2.5 fusion.109
  58.1 10.7 %all_gather.31 = bf16[1024,256]{1,0:T(8,128)(2,1)} all-gather(bf16[128,256]{1,0:T(8,128)(2,1)S(1)} %get-tuple-element.39), channel_id=1, replica_groups=mesh['seq'=8,'head'=4] {'seq'}, dimensions={0}, use_global_device_ids=true | all-gather | bytes 589824 | tf_op jit(solution)/shard_map/all_gather | solution.py:76
  70.1 2.2 fusion.12
  73.8 52.3 %all-reduce.5.cloned.1.call-done = f32[256,1024]{1,0:T(8,128)} async-done(((f32[256,1024]{1,0:T(8,128)}), f32[256,1024]{1,0:T(8,128)}) %all-reduce.5.cloned.1.call-update) | async-done | bytes 1048592 | tf_op jit(solution)/shard_map/psum | solution.py:134
  132.3 51.3 %all-reduce.7.cloned.1.call-done = f32[256,1024]{1,0:T(8,128)} async-done(((f32[256,1024]{1,0:T(8,128)}), f32[256,1024]{1,0:T(8,128)}) %all-reduce.7.cloned.1.call-update) | async-done | bytes 1048592 | tf_op jit(solution)/shard_map/psum | solution.py:144
  187.7 11.0 %all_gather.33 = bf16[1024,256]{1,0:T(8,128)(2,1)} all-gather(bf16[128,256]{1,0:T(8,128)(2,1)S(1)} %get-tuple-element.36), channel_id=1, replica_groups=mesh['seq'=8,'head'=4] {'seq'}, dimensions={0}, use_global_device_ids=true | all-gather | bytes 589824 | tf_op jit(solution)/shard_map/all_gather | solution.py:55
  198.7 2.0 copy.32
  201.7 2.9 multiply_reduce_fusion
  206.3 10.7 %all_gather.34 = bf16[1024,256]{1,0:T(8,128)(2,1)} all-gather(bf16[128,256]{1,0:T(8,128)(2,1)S(1)} %get-tuple-element.35), channel_id=1, replica_groups=mesh['seq'=8,'head'=4] {'seq'}, dimensions={0}, use_global_device_ids=true | all-gather | bytes 589824 | tf_op jit(solution)/shard_map/all_gather | solution.py:75
  217.0 2.1 copy.33
  220.6 9.9 %all_gather.32 = bf16[1024,256]{1,0:T(8,128)(2,1)} all-gather(bf16[128,256]{1,0:T(8,128)(2,1)S(1)} %get-tuple-element.34), channel_id=1, replica_groups=mesh['seq'=8,'head'=4] {'seq'}, dimensions={0}, use_global_device_ids=true | all-gather | bytes 589824 | tf_op jit(solution)/shard_map/all_gather | solution.py:56
  230.5 2.1 copy.31
  232.6 2.2 fusion.2
  234.8 2.7 fusion.111
  240.5 10.7 %all_gather.35 = bf16[1024,256]{1,0:T(8,128)(2,1)} all-gather(bf16[128,256]{1,0:T(8,128)(2,1)S(1)} %copy-done.16), channel_id=1, replica_groups=mesh['seq'=8,'head'=4] {'seq'}, dimensions={0}, use_global_device_ids=true | all-gather | bytes 589824 | tf_op jit(solution)/shard_map/all_gather | solution.py:76
  253.2 2.4 fusion.13
  257.1 50.3 %all-reduce.9.cloned.1.call-done = f32[256,1024]{1,0:T(8,128)} async-done(((f32[256,1024]{1,0:T(8,128)}), f32[256,1024]{1,0:T(8,128)}) %all-reduce.9.cloned.1.call-update) | async-done | bytes 1048592 | tf_op jit(solution)/shard_map/psum | solution.py:134
  312.9 51.3 %all-reduce.11.cloned.1.call-done = f32[256,1024]{1,0:T(8,128)} async-done(((f32[256,1024]{1,0:T(8,128)}), f32[256,1024]{1,0:T(8,128)}) %all-reduce.11.cloned.1.call-update) | async-done | bytes 1048592 | tf_op jit(solution)/shard_map/psum | solution.py:144
  364.2 2.5 multiply_reduce_fusion.2
  367.8 14.3 %psum.39 = f32[]{:T(128)} all-reduce(f32[]{:T(128)} %get-tuple-element.13), channel_id=1, replica_groups=mesh['seq'=8,'head'=4] {'seq'}, use_global_device_ids=true, to_apply=%region_22.0 | all-reduce | flops 1 | bytes 8 | tf_op jit(solution)/shard_map/psum | solution.py:166
  (107 shorter events, 45.1 us)
Async XLA Ops:
  7.2 121.8 %copy-start = (bf16[1024,1024]{1,0:T(8,128)(2,1)S(1)}, bf16[1024,1024]{1,0:T(8,128)(2,1)}, u32[]{:S(2)}) copy-start(bf16[1024,1024]{1,0:T(8,128)(2,1)} %param.20) | copy-start | bytes 6291460
  7.2 118.9 %all-reduce.5.cloned.1.call-start = ((), (), s32[]{:S(2)}) async-start(), calls=%async_computation | async-start | bytes 2097152 | tf_op jit(solution)/shard_map/psum | solution.py:134
  10.7 13.1 %copy-start.14 = (bf16[128,1024]{1,0:T(8,128)(2,1)}, bf16[128,1024]{1,0:T(8,128)(2,1)S(1)}, u32[]{:S(2)}) copy-start(bf16[128,1024]{1,0:T(8,128)(2,1)S(1)} %get-tuple-element.31) | copy-start | bytes 786436
  51.6 2.2 copy-start.1
  68.8 3.5 copy-start.12
  72.3 53.7 %copy-start.3 = (bf16[128,1024]{1,0:T(8,128)(2,1)S(1)}, bf16[128,1024]{1,0:T(8,128)(2,1)}, u32[]{:S(2)}) copy-start(bf16[128,1024]{1,0:T(8,128)(2,1)} %param.12) | copy-start | bytes 786436
  72.4 55.3 %copy-start.19 = (f32[1024]{0:T(1024)S(1)}, f32[1024]{0:T(1024)}, u32[]{:S(2)}) copy-start(f32[1024]{0:T(1024)} %param.19) | copy-start | bytes 12292
  73.7 109.8 %all-reduce.7.cloned.1.call-start = ((), (), s32[]{:S(2)}) async-start(), calls=%async_computation.1 | async-start | bytes 2097152 | tf_op jit(solution)/shard_map/psum | solution.py:144
  126.1 1.6 copy-start.4
  132.2 52.8 %copy-start.18 = (f32[1024]{0:T(1024)S(1)}, f32[1024]{0:T(1024)}, u32[]{:S(2)}) copy-start(f32[1024]{0:T(1024)} %param.14) | copy-start | bytes 12292
  132.3 175.1 %all-reduce.9.cloned.1.call-start = ((), (), s32[]{:S(2)}) async-start(), calls=%async_computation.2 | async-start | bytes 2097152 | tf_op jit(solution)/shard_map/psum | solution.py:134
  183.6 1.8 copy-start.20
  183.6 2.1 copy-start.21
  185.0 1.7 copy-start.7
  185.1 1.6 copy-start.22
  200.7 3.8 copy-start.11
  232.6 2.2 copy-start.2
  234.8 3.4 copy-start.10
  238.2 2.3 copy-start.16
  253.2 2.4 copy-start.13
  253.2 2.4 copy-start.17
  257.0 107.2 %all-reduce.11.cloned.1.call-start = ((), (), s32[]{:S(2)}) async-start(), calls=%async_computation.3 | async-start | bytes 2097152 | tf_op jit(solution)/shard_map/psum | solution.py:144
  307.4 1.9 copy-start.9
  311.2 53.0 %copy-start.8 = (f32[128,1024]{1,0:T(8,128)S(1)}, f32[128,1024]{1,0:T(8,128)}, u32[]{:S(2)}) copy-start(f32[128,1024]{1,0:T(8,128)} %copy-done.7) | copy-start | bytes 1572868
  (3 other events, 4.8 us)
Sparse Core Ops, SparseCore 0:
  73.9 52.1 all-reduce.4
  132.4 51.1 all-reduce.6
  257.1 50.2 all-reduce.8
  313.0 51.1 all-reduce.10
where the time goes:
time: 391 us; the launch traced here: 390 us
  waiting for transfers between devices  205 us (52%)
  blocking collectives  98.5 us (25%)
  matrix products  35.8 us (9%)
  other arithmetic  20.1 us (5%)
  between operations  16 us (4%)
  local copies, waits for them, and re-layouts  14.7 us (4%)
    psum x2, waiting for transfers between devices, whole_field(): attn_both = lax.psum(attn_terms, 'head')  103 us
    psum x2, waiting for transfers between devices, whole_field(): mlp_both = lax.psum(mlp_terms, 'head')  103 us
    all_gather x2, blocking collectives, attention(): lax.all_gather(keys, 'seq', axis=0, tiled=True)  22.4 us
    all_gather x2, blocking collectives, attention(): lax.all_gather(val_tang, 'seq', axis=0, tiled=True)  21.4 us
    all_gather x2, blocking collectives, attention(): lax.all_gather(key_tang, 'seq', axis=0, tiled=True)  20.5 us
    all_gather x2, blocking collectives, attention(): lax.all_gather(vals, 'seq', axis=0, tiled=True)  19.9 us
    psum x1, blocking collectives, per_device(): grand_total = lax.psum(jnp.sum(frame_logp), 'seq')  14.3 us
  transfers between devices with their start and end apart: 4, of which 4 were waited for; matrix products, arithmetic and copies ran while one was open for 0% of the time, Pallas kernels for 0%

commit v1 on v0

--- a/solution.py
+++ b/solution.py
@@ -141,7 +141,10 @@
     mlp_terms = jnp.dot(
         jnp.concatenate([activ, activ_tang], axis=0), w_down, preferred_element_type=jnp.float32
     )
-    mlp_both = lax.psum(mlp_terms, "head")
+    size, mlp_both = (lax.axis_size("head"), mlp_terms)
+    for far in [1 << k for k in range(size.bit_length() - 1)]:
+        route = [(i, i ^ far) for i in range(size)]
+        mlp_both = mlp_both + lax.ppermute(mlp_both, "head", route)
     return (attn + mlp_both[:rows], attn_tang + mlp_both[rows:])
 
 

time: 391 us -> 430 us (1.100)
  waiting for transfers between devices: 205 us -> 241 us
  starting transfers between devices: 0.16 us -> 5.44 us
    ppermute x0 -> x4, waiting for transfers between devices: none -> 138 us  [whole_field(): mlp_both = mlp_both + lax.ppermute(mlp_both, 'head', route)]
    psum x2 -> x0, waiting for transfers between devices: 103 us -> none  [whole_field(): mlp_both = lax.psum(mlp_terms, 'head')]
    ppermute x0 -> x4, starting transfers between devices: none -> 5.18 us  [whole_field(): mlp_both = mlp_both + lax.ppermute(mlp_both, 'head', route)]
  transfers between devices with their start and end apart: 4 -> 6, of which waited for: 4 -> 6; matrix products, arithmetic and copies ran while one was open for 0% -> 0% of each run, Pallas kernels for 0% -> 0%
where the time goes in v1:
time: 430 us; the launch traced here: 429 us
  waiting for transfers between devices  241 us (56%)
  blocking collectives  98.7 us (23%)
  matrix products  33.8 us (8%)
  other arithmetic  18.1 us (4%)
  between operations  16.3 us (4%)
  local copies, waits for them, and re-layouts  15.6 us (4%)
  starting transfers between devices  5.44 us (1%)
    ppermute x4, waiting for transfers between devices, whole_field(): mlp_both = mlp_both + lax.ppermute(mlp_both, 'head', route)  138 us
    psum x2, waiting for transfers between devices, whole_field(): attn_both = lax.psum(attn_terms, 'head')  103 us
    all_gather x2, blocking collectives, attention(): lax.all_gather(keys, 'seq', axis=0, tiled=True)  22.2 us
    all_gather x2, blocking collectives, attention(): lax.all_gather(val_tang, 'seq', axis=0, tiled=True)  21.6 us
    all_gather x2, blocking collectives, attention(): lax.all_gather(key_tang, 'seq', axis=0, tiled=True)  20.5 us
    all_gather x2, blocking collectives, attention(): lax.all_gather(vals, 'seq', axis=0, tiled=True)  19.9 us
    psum x1, blocking collectives, per_device(): grand_total = lax.psum(jnp.sum(frame_logp), 'seq')  14.5 us
  transfers between devices with their start and end apart: 6, of which 6 were waited for; matrix products, arithmetic and copies ran while one was open for 0% of the time, Pallas kernels for 0%

profile of v1, /device:TPU:0, one launch (start us, length us, event | category | flops | bytes accessed | tf_op | source)
XLA Modules:
  0.0 429.3 jit_solution(13410805094121252881)
XLA Ops:
  12.2 11.3 %all_gather.29 = bf16[1024,256]{1,0:T(8,128)(2,1)S(1)} all-gather(bf16[128,256]{1,0:T(8,128)(2,1)S(1)} %get-tuple-element.42), channel_id=1, replica_groups=mesh['seq'=8,'head'=4] {'seq'}, dimensions={0}, use_global_device_ids=true | all-gather | bytes 589824 | tf_op jit(solution)/shard_map/all_gather | solution.py:55
  28.9 9.8 %all_gather.30 = bf16[1024,256]{1,0:T(8,128)(2,1)S(1)} all-gather(bf16[128,256]{1,0:T(8,128)(2,1)S(1)} %get-tuple-element.41), channel_id=1, replica_groups=mesh['seq'=8,'head'=4] {'seq'}, dimensions={0}, use_global_device_ids=true | all-gather | bytes 589824 | tf_op jit(solution)/shard_map/all_gather | solution.py:75
  40.4 9.9 %all_gather.28 = bf16[1024,256]{1,0:T(8,128)(2,1)} all-gather(bf16[128,256]{1,0:T(8,128)(2,1)S(1)} %get-tuple-element.40), channel_id=1, replica_groups=mesh['seq'=8,'head'=4] {'seq'}, dimensions={0}, use_global_device_ids=true | all-gather | bytes 589824 | tf_op jit(solution)/shard_map/all_gather | solution.py:56
  51.6 2.2 fusion
  53.9 2.5 fusion.109
  58.1 10.7 %all_gather.31 = bf16[1024,256]{1,0:T(8,128)(2,1)} all-gather(bf16[128,256]{1,0:T(8,128)(2,1)S(1)} %get-tuple-element.39), channel_id=1, replica_groups=mesh['seq'=8,'head'=4] {'seq'}, dimensions={0}, use_global_device_ids=true | all-gather | bytes 589824 | tf_op jit(solution)/shard_map/all_gather | solution.py:76
  70.1 2.2 fusion.12
  74.0 52.1 %all-reduce.3.cloned.1.call-done = f32[256,1024]{1,0:T(8,128)} async-done(((f32[256,1024]{1,0:T(8,128)}), f32[256,1024]{1,0:T(8,128)}) %all-reduce.3.cloned.1.call-update) | async-done | bytes 1048592 | tf_op jit(solution)/shard_map/psum | solution.py:134
  132.6 23.7 %collective-permute-done = f32[256,1024]{1,0:T(8,128)S(1)} collective-permute-done((f32[256,1024]{1,0:T(8,128)S(1)}, f32[256,1024]{1,0:T(8,128)S(1)}, u32[]{:S(2)}, u32[]{:S(2)}) %collective-permute-start) | collective-permute-done | bytes 1048608 | tf_op jit(solution)/shard_map/ppermute | solution.py:147
  157.7 45.4 %collective-permute-done.1 = f32[256,1024]{1,0:T(8,128)S(1)} collective-permute-done((f32[256,1024]{1,0:T(8,128)S(1)}, f32[256,1024]{1,0:T(8,128)S(1)}, u32[]{:S(2)}, u32[]{:S(2)}) %collective-permute-start.1) | collective-permute-done | bytes 1048608 | tf_op jit(solution)/shard_map/ppermute | solution.py:147
  207.0 10.9 %all_gather.33 = bf16[1024,256]{1,0:T(8,128)(2,1)} all-gather(bf16[128,256]{1,0:T(8,128)(2,1)S(1)} %get-tuple-element.36), channel_id=1, replica_groups=mesh['seq'=8,'head'=4] {'seq'}, dimensions={0}, use_global_device_ids=true | all-gather | bytes 589824 | tf_op jit(solution)/shard_map/all_gather | solution.py:55
  220.9 2.9 multiply_reduce_fusion
  225.5 10.7 %all_gather.34 = bf16[1024,256]{1,0:T(8,128)(2,1)} all-gather(bf16[128,256]{1,0:T(8,128)(2,1)S(1)} %get-tuple-element.35), channel_id=1, replica_groups=mesh['seq'=8,'head'=4] {'seq'}, dimensions={0}, use_global_device_ids=true | all-gather | bytes 589824 | tf_op jit(solution)/shard_map/all_gather | solution.py:75
  236.3 2.1 copy.33
  239.8 9.9 %all_gather.32 = bf16[1024,256]{1,0:T(8,128)(2,1)} all-gather(bf16[128,256]{1,0:T(8,128)(2,1)S(1)} %get-tuple-element.34), channel_id=1, replica_groups=mesh['seq'=8,'head'=4] {'seq'}, dimensions={0}, use_global_device_ids=true | all-gather | bytes 589824 | tf_op jit(solution)/shard_map/all_gather | solution.py:56
  249.8 2.0 copy.31
  251.8 2.2 fusion.2
  254.0 2.8 fusion.111
  259.7 10.9 %all_gather.35 = bf16[1024,256]{1,0:T(8,128)(2,1)} all-gather(bf16[128,256]{1,0:T(8,128)(2,1)S(1)} %copy-done.18), channel_id=1, replica_groups=mesh['seq'=8,'head'=4] {'seq'}, dimensions={0}, use_global_device_ids=true | all-gather | bytes 589824 | tf_op jit(solution)/shard_map/all_gather | solution.py:76
  272.7 2.4 fusion.13
  276.4 51.1 %all-reduce.5.cloned.1.call-done = f32[256,1024]{1,0:T(8,128)} async-done(((f32[256,1024]{1,0:T(8,128)}), f32[256,1024]{1,0:T(8,128)}) %all-reduce.5.cloned.1.call-update) | async-done | bytes 1048592 | tf_op jit(solution)/shard_map/psum | solution.py:134
  333.5 23.7 %collective-permute-done.2 = f32[256,1024]{1,0:T(8,128)S(1)} collective-permute-done((f32[256,1024]{1,0:T(8,128)S(1)}, f32[256,1024]{1,0:T(8,128)S(1)}, u32[]{:S(2)}, u32[]{:S(2)}) %collective-permute-start.2) | collective-permute-done | bytes 1048608 | tf_op jit(solution)/shard_map/ppermute | solution.py:147
  358.5 45.4 %collective-permute-done.3 = f32[256,1024]{1,0:T(8,128)S(1)} collective-permute-done((f32[256,1024]{1,0:T(8,128)S(1)}, f32[256,1024]{1,0:T(8,128)S(1)}, u32[]{:S(2)}, u32[]{:S(2)}) %collective-permute-start.3) | collective-permute-done | bytes 1048608 | tf_op jit(solution)/shard_map/ppermute | solution.py:147
  406.2 14.5 %psum.23 = f32[]{:T(128)} all-reduce(f32[]{:T(128)} %get-tuple-element.13), channel_id=1, replica_groups=mesh['seq'=8,'head'=4] {'seq'}, use_global_device_ids=true, to_apply=%region_20.0 | all-reduce | flops 1 | bytes 8 | tf_op jit(solution)/shard_map/psum | solution.py:169
  (117 shorter events, 51.7 us)
Async XLA Ops:
  7.2 121.8 %copy-start = (bf16[1024,1024]{1,0:T(8,128)(2,1)S(1)}, bf16[1024,1024]{1,0:T(8,128)(2,1)}, u32[]{:S(2)}) copy-start(bf16[1024,1024]{1,0:T(8,128)(2,1)} %param.20) | copy-start | bytes 6291460
  7.2 118.9 %all-reduce.3.cloned.1.call-start = ((), (), s32[]{:S(2)}) async-start(), calls=%async_computation | async-start | bytes 2097152 | tf_op jit(solution)/shard_map/psum | solution.py:134
  10.7 13.1 %copy-start.16 = (bf16[128,1024]{1,0:T(8,128)(2,1)}, bf16[128,1024]{1,0:T(8,128)(2,1)S(1)}, u32[]{:S(2)}) copy-start(bf16[128,1024]{1,0:T(8,128)(2,1)S(1)} %get-tuple-element.31) | copy-start | bytes 786436
  51.6 2.2 copy-start.1
  68.8 3.5 copy-start.14
  72.3 53.7 %copy-start.3 = (bf16[128,1024]{1,0:T(8,128)(2,1)S(1)}, bf16[128,1024]{1,0:T(8,128)(2,1)}, u32[]{:S(2)}) copy-start(bf16[128,1024]{1,0:T(8,128)(2,1)} %param.12) | copy-start | bytes 786436
  72.4 55.3 %copy-start.21 = (f32[1024]{0:T(1024)S(1)}, f32[1024]{0:T(1024)}, u32[]{:S(2)}) copy-start(f32[1024]{0:T(1024)} %param.19) | copy-start | bytes 12292
  73.7 253.8 %all-reduce.5.cloned.1.call-start = ((), (), s32[]{:S(2)}) async-start(), calls=%async_computation.1 | async-start | bytes 2097152 | tf_op jit(solution)/shard_map/psum | solution.py:134
  131.2 25.1 %collective-permute-start = (f32[256,1024]{1,0:T(8,128)S(1)}, f32[256,1024]{1,0:T(8,128)S(1)}, u32[]{:S(2)}, u32[]{:S(2)}) collective-permute-start(f32[256,1024]{1,0:T(8,128)S(1)} %fusion.61), channel_id=1, source_target_pairs={{0,1},{1,0},{2,3},{3,2},{4,5},{5,4},{6,7},{7,6},{8,9},{9,8},{10,11... | collective-permute-start | bytes 3145736 | tf_op jit(solution)/shard_map/ppermute | solution.py:147
  156.5 46.8 %copy-start.10 = (bf16[128,1024]{1,0:T(8,128)(2,1)S(1)}, bf16[128,1024]{1,0:T(8,128)(2,1)}, u32[]{:S(2)}) copy-start(bf16[128,1024]{1,0:T(8,128)(2,1)} %param.11) | copy-start | bytes 786436
  156.5 47.1 %copy-start.20 = (f32[1024]{0:T(1024)S(1)}, f32[1024]{0:T(1024)}, u32[]{:S(2)}) copy-start(f32[1024]{0:T(1024)} %param.14) | copy-start | bytes 12292
  156.5 46.6 %collective-permute-start.1 = (f32[256,1024]{1,0:T(8,128)S(1)}, f32[256,1024]{1,0:T(8,128)S(1)}, u32[]{:S(2)}, u32[]{:S(2)}) collective-permute-start(f32[256,1024]{1,0:T(8,128)S(1)} %add.170), channel_id=1, source_target_pairs={{0,2},{1,3},{2,0},{3,1},{4,6},{5,7},{6,4},{7,5},{8,10},{9,11},{10,... | collective-permute-start | bytes 3145736 | tf_op jit(solution)/shard_map/ppermute | solution.py:147
  203.5 2.5 copy-start.7
  203.6 2.4 copy-start.24
  220.0 3.8 copy-start.12
  251.8 2.2 copy-start.2
  254.0 3.4 copy-start.11
  257.4 2.3 copy-start.18
  272.7 2.4 copy-start.15
  272.7 2.4 copy-start.19
  327.6 1.9 copy-start.9
  332.1 25.1 %collective-permute-start.2 = (f32[256,1024]{1,0:T(8,128)S(1)}, f32[256,1024]{1,0:T(8,128)S(1)}, u32[]{:S(2)}, u32[]{:S(2)}) collective-permute-start(f32[256,1024]{1,0:T(8,128)S(1)} %fusion.69), channel_id=1, source_target_pairs={{0,1},{1,0},{2,3},{3,2},{4,5},{5,4},{6,7},{7,6},{8,9},{9,8},{10,11... | collective-permute-start | bytes 3145736 | tf_op jit(solution)/shard_map/ppermute | solution.py:147
  357.3 46.7 %copy-start.8 = (f32[128,1024]{1,0:T(8,128)S(1)}, f32[128,1024]{1,0:T(8,128)}, u32[]{:S(2)}) copy-start(f32[128,1024]{1,0:T(8,128)} %copy-done.7) | copy-start | bytes 1572868
  357.3 46.6 %collective-permute-start.3 = (f32[256,1024]{1,0:T(8,128)S(1)}, f32[256,1024]{1,0:T(8,128)S(1)}, u32[]{:S(2)}, u32[]{:S(2)}) collective-permute-start(f32[256,1024]{1,0:T(8,128)S(1)} %add.187), channel_id=1, source_target_pairs={{0,2},{1,3},{2,0},{3,1},{4,6},{5,7},{6,4},{7,5},{8,10},{9,11},{10,... | collective-permute-start | bytes 3145736 | tf_op jit(solution)/shard_map/ppermute | solution.py:147
  (7 other events, 11.3 us)
Sparse Core Ops, SparseCore 0:
  73.9 52.1 all-reduce.2
  276.6 50.9 all-reduce.4
